TPU v7x, 8 devices: a whole 2x2x1 slice. The times are simulated.
8 devices in a mesh: dp: 1 (over z), sp: 8 (over x, y, core).
Axes of the slice: x: 2, y: 2, z: 1, core: 2. Of those that a mesh axis runs over, the one named last changes fastest.
Arguments:
- q: bfloat16 [32, 56, 128], P('dp')
- k: bfloat16 [32, 2048, 56, 128], P('dp', 'sp')
- v: bfloat16 [32, 2048, 56, 128], P('dp', 'sp')
Outputs:
- q: bfloat16 [32, 56, 128], P('dp')
All inputs are finite; a program needn't handle non-finite values.
Results may differ from a plain program's by a relative error of at most 0.012.
Values are sent between devices in bfloat16 or wider.
A program may use at most 2 GiB of HBM per device.

v0:
```python
import jax
import jax.numpy as jnp
from jax import lax
from jax.sharding import PartitionSpec as P


def einsum(form, a, b):
    return jnp.einsum(form, a.astype(jnp.float32), b.astype(jnp.float32))


def part_of(q, k, v):
    grouped = q.reshape(q.shape[0], k.shape[2], -1, q.shape[2])
    scores = einsum("bgsd,bugd->bgsu", grouped, k) * q.shape[2] ** -0.5
    high = jnp.max(scores, -1, keepdims=True)
    weights = jnp.exp(scores - high)
    seen = einsum("bgsu,bugd->bgsd", weights.astype(jnp.bfloat16), v)
    return jnp.concatenate([seen, jnp.sum(weights, -1, keepdims=True), high], -1)


def together(parts):
    seen, total, high = parts[..., :-2], parts[..., -2:-1], parts[..., -1:]
    scale = jnp.exp(high - jnp.max(high, 0))
    return (jnp.sum(seen * scale, 0) / jnp.sum(total * scale, 0)).astype(jnp.bfloat16)


def solution(mesh):
    def step(q, k, v):
        return together(lax.all_gather(part_of(q, k, v), "sp")).reshape(q.shape)

    return jax.shard_map(
        step,
        mesh=mesh,
        in_specs=(P("dp", None, None), P("dp", "sp", None, None), P("dp", "sp", None, None)),
        out_specs=P("dp", None, None),
        check_vma=False,
    )
```

profile of v0, /device:TPU:0, one launch (start us, length us, event | category | flops | bytes accessed | tf_op | source)
XLA Modules:
  0.0 203.1 jit_solution(11696820149718696094)
XLA Ops:
  6.5 0.0 all-gather.3.cloned.1.call-start
  6.5 42.6 %fusion.2 = f32[32,56,1,256]{3,2,1,0:T(1,128)S(1)} fusion(bf16[32,256,56,128]{3,2,1,0:T(8,128)(2,1)} %param.4, bf16[32,56,128,1]{2,1,0,3:T(8,128)(2,1)} %bitcast.22), kind=kOutput, calls=%fused_computation.2 | convolution fusion | flops 117440512 | bytes 119734272 | tf_op jit(solution)/shard_map/bgsd,bugd->bgsu/dot_general | solution.py:8
  49.1 0.3 fusion.8
  49.4 0.7 fusion.9
  50.1 42.4 %fusion = f32[32,56,1,128]{3,2,1,0:T(1,128)S(1)} fusion(bf16[32,256,56,128]{3,2,1,0:T(8,128)(2,1)} %param.5, bf16[32,56,256,1]{2,1,0,3:T(8,128)(2,1)S(1)} %get-tuple-element.7), kind=kOutput, calls=%fused_computation | convolution fusion | flops 117440512 | bytes 119275520 | tf_op jit(solution)/shard_map/bgsu,bugd->bgsd/dot_general | solution.py:8
  92.5 1.4 copy.12
  93.9 1.6 pad_maximum_fusion
  95.5 0.0 all-gather.3.cloned.1.call-update
  95.5 88.2 %all-gather.3.cloned.1.call-done = f32[256,56,1,130]{1,0,3,2:T(8,128)} async-done(((f32[32,56,1,130]{1,0,3,2:T(8,128)}), f32[256,56,1,130]{1,0,3,2:T(8,128)}) %all-gather.3.cloned.1.call-update) | async-done | bytes 7454736 | tf_op jit(solution)/shard_map/all_gather | solution.py:28
  183.7 0.9 slice_reduce_fusion
  184.6 1.0 fusion.11
  185.6 8.6 %fusion.4 = f32[32,56,128]{1,0,2:T(8,128)S(1)} fusion(f32[8,32,56,1,130]{2,1,0,4,3:T(8,128)} %bitcast.21, f32[8,32,56]{2,1,0:T(8,128)S(1)} %get-tuple-element.6), kind=kLoop, calls=%fused_computation.5 | loop fusion | flops 3440640 | bytes 8314880 | tf_op jit(solution)/shard_map/reduce_sum | solution.py:23
  194.2 0.2 divide_convert_fusion
  194.5 1.8 copy.6
Async XLA Ops:
  6.5 177.1 %all-gather.3.cloned.1.call-start = ((), (), s32[]{:S(2)}) async-start(), calls=%async_computation | async-start | bytes 19169280 | tf_op jit(solution)/shard_map/all_gather | solution.py:28
Sparse Core Ops, SparseCore 0:
  95.6 88.0 all-gather.2
where the time goes:
time: 204 us; the launch traced here: 203 us
  waiting for transfers between devices  88.2 us (43%)
  matrix products  85 us (42%)
  other arithmetic  13.4 us (7%)
  between operations  13.4 us (7%)
  local copies, waits for them, and re-layouts  3.2 us (2%)
    all_gather x1, waiting for transfers between devices, step(): return together(lax.all_gather(part_of(q, k, v), 'sp')).reshape(q.shape)  88.2 us
    dot_general x2, matrix products, einsum(): return jnp.einsum(form, a.astype(jnp.float32), b.astype(jnp.float32))  85 us
    reduce_sum x1, other arithmetic, together(): jnp.sum(seen * scale, 0) / jnp.sum(total * scale, 0)  8.59 us
  transfers between devices with their start and end apart: 1, of which 1 were waited for; matrix products, arithmetic and copies ran while one was open for 0% of the time, Pallas kernels for 0%

commit v1 on v0

v1 whole, which is shorter than its diff:
```python
import functools

import jax
import jax.numpy as jnp
from jax import lax
from jax.experimental import pallas as pl
from jax.experimental.pallas import tpu as pltpu
from jax.sharding import PartitionSpec as P

MESH = pl.DeviceIdType.MESH
LOG2E = 1.4426950408889634
SLOTS = 4
LAG = 4
ROWS = 16


def kernel(n, q_hbm, k_hbm, v_hbm, o_hbm, kbuf, vbuf, qbuf, part, stat, out, ksem, vsem, qsem, osem, send_sem, recv_sem):
    batch, pairs, groups, rows, head = k_hbm.shape
    heads = q_hbm.shape[1]
    half = pairs // 2
    tiles = heads // 8
    me = lax.axis_index("sp")
    dp = lax.axis_index("dp")
    scale = head**-0.5 * LOG2E

    def fetch(b, slot):
        return (
            pltpu.make_async_copy(k_hbm.at[b], kbuf.at[slot], ksem.at[slot]),
            pltpu.make_async_copy(v_hbm.at[b], vbuf.at[slot], vsem.at[slot]),
        )

    q_copy = pltpu.make_async_copy(q_hbm, qbuf, qsem)
    q_copy.start()
    for slot in range(SLOTS):
        for copy in fetch(slot, slot):
            copy.start()

    barrier = pltpu.get_barrier_semaphore()
    for i in range(1, n):
        pl.semaphore_signal(barrier, inc=1, device_id=(dp, lax.rem(me + i, n)), device_id_type=MESH)
    q_copy.wait()
    pl.semaphore_wait(barrier, n - 1)

    def sends(b, i):
        peer = (dp, lax.rem(me + i, n))
        return [
            pltpu.make_async_remote_copy(
                src_ref=ref.at[me, b],
                dst_ref=ref.at[me, b],
                send_sem=send_sem.at[x],
                recv_sem=recv_sem.at[x, b],
                device_id=peer,
                device_id_type=MESH,
            )
            for x, ref in enumerate((part, stat))
        ]

    def attend(b, slot):
        q32 = qbuf[b].astype(jnp.float32)
        qq = jnp.concatenate([q32, q32], 0)
        row = lax.broadcasted_iota(jnp.int32, (2 * ROWS, half * ROWS), 0) % ROWS
        col = lax.broadcasted_iota(jnp.int32, (2 * ROWS, half * ROWS), 1) % ROWS
        own = row == col
        zero = jnp.zeros((ROWS, head), jnp.bfloat16)
        sums, highs, totals = [], [], []
        for j in range(groups):
            q16 = qq[ROWS * j : ROWS * (j + 1)].astype(jnp.bfloat16)
            lhs = jnp.concatenate([jnp.concatenate([q16, zero], 1), jnp.concatenate([zero, q16], 1)], 0)
            keys = [kbuf[slot, half * a : half * (a + 1), j].reshape(half * ROWS, head) for a in range(2)]
            s = lax.dot_general(
                lhs, jnp.concatenate(keys, 1), (((1,), (1,)), ((), ())), preferred_element_type=jnp.float32
            )
            s = jnp.where(own, s, -jnp.inf)
            high = jnp.max(s, 1, keepdims=True)
            high = jnp.maximum(high[:ROWS], high[ROWS:])
            p = jnp.exp2((s - jnp.concatenate([high, high], 0)) * scale)
            total = jnp.sum(p, 1, keepdims=True)
            values = [vbuf[slot, half * a : half * (a + 1), j].reshape(half * ROWS, head) for a in range(2)]
            o = jnp.dot(p.astype(jnp.bfloat16), jnp.concatenate(values, 1), preferred_element_type=jnp.float32)
            o = o[:ROWS, :head] + o[ROWS:, head:]
            total = total[:ROWS] + total[ROWS:]
            for t in range(ROWS // 8):
                rows8 = slice(8 * t, 8 * (t + 1))
                sums.append(o[rows8])
                highs.append(high[rows8])
                totals.append(total[rows8])
        lane = lax.broadcasted_iota(jnp.int32, (8, head), 1)
        tile = jnp.zeros((8, head), jnp.float32)
        seen = []
        for g in range(tiles):
            high = jnp.maximum(highs[g], highs[g + tiles])
            e0 = jnp.exp2((highs[g] - high) * scale)
            e1 = jnp.exp2((highs[g + tiles] - high) * scale)
            seen.append(sums[g] * e0 + sums[g + tiles] * e1)
            tile = jnp.where(lane == g, high, tile)
            tile = jnp.where(lane == g + 8, totals[g] * e0 + totals[g + tiles] * e1, tile)
        part[me, b] = jnp.concatenate(seen, 0).astype(jnp.bfloat16)
        stat[me, b] = tile

    def together(b):
        for x, ref in enumerate((part, stat)):
            peers = ref.at[pl.ds(0, n - 1), b]
            pltpu.make_async_copy(peers, peers, recv_sem.at[x, b]).wait()
        stats = [stat[i, b] for i in range(n)]
        high = functools.reduce(jnp.maximum, stats)
        weights = [jnp.exp2((s - high) * scale) for s in stats]
        total = sum(w * pltpu.roll(s, head - 8, 1) for w, s in zip(weights, stats))
        weights = [w / total for w in weights]
        acc = [jnp.zeros((8, head), jnp.float32)] * tiles
        for i in range(n):
            mine = part[i, b].astype(jnp.float32)
            for g in range(tiles):
                acc[g] = acc[g] + mine[8 * g : 8 * (g + 1)] * weights[i][:, g : g + 1]
        out[b] = jnp.concatenate(acc, 0).astype(jnp.bfloat16)
        pltpu.make_async_copy(out.at[b], o_hbm.at[b], osem).start()

    def step(b, _):
        slot = lax.rem(b, SLOTS)
        for copy in fetch(b, slot):
            copy.wait()
        attend(b, slot)
        for i in range(1, n):
            for copy in sends(b, i):
                copy.start()

        @pl.when(b + SLOTS < batch)
        def _():
            for copy in fetch(b + SLOTS, slot):
                copy.start()

        @pl.when(b >= LAG)
        def _():
            together(b - LAG)

        return 0

    lax.fori_loop(0, batch, step, 0)
    lax.fori_loop(batch - LAG, batch, lambda b, _: (together(b), 0)[1], 0)

    for x, ref in enumerate((part, stat)):
        peers = ref.at[pl.ds(0, n - 1)]
        pltpu.make_async_copy(peers, peers, send_sem.at[x]).wait()
    pltpu.make_async_copy(out, o_hbm, osem).wait()


def solution(mesh):
    n = mesh.shape["sp"]

    def step(q, k, v):
        batch, heads, head = q.shape
        tokens = k.shape[1]
        groups = 2 * heads // ROWS
        shape = (batch, tokens // 2, groups, ROWS, head)
        return pl.pallas_call(
            functools.partial(kernel, n),
            out_shape=jax.ShapeDtypeStruct(q.shape, q.dtype),
            in_specs=[pl.BlockSpec(memory_space=pl.ANY)] * 3,
            out_specs=pl.BlockSpec(memory_space=pl.ANY),
            scratch_shapes=[
                pltpu.VMEM((SLOTS,) + shape[1:], jnp.bfloat16),
                pltpu.VMEM((SLOTS,) + shape[1:], jnp.bfloat16),
                pltpu.VMEM(q.shape, jnp.bfloat16),
                pltpu.VMEM((n, batch, heads, head), jnp.bfloat16),
                pltpu.VMEM((n, batch, 8, head), jnp.float32),
                pltpu.VMEM(q.shape, jnp.bfloat16),
                pltpu.SemaphoreType.DMA((SLOTS,)),
                pltpu.SemaphoreType.DMA((SLOTS,)),
                pltpu.SemaphoreType.DMA,
                pltpu.SemaphoreType.DMA,
                pltpu.SemaphoreType.DMA((2,)),
                pltpu.SemaphoreType.DMA((2, batch)),
            ],
            compiler_params=pltpu.CompilerParams(
                collective_id=0, has_side_effects=True, vmem_limit_bytes=60 * 1024 * 1024
            ),
        )(q, k.reshape(shape), v.reshape(shape))

    return jax.shard_map(
        step,
        mesh=mesh,
        in_specs=(P("dp", None, None), P("dp", "sp", None, None), P("dp", "sp", None, None)),
        out_specs=P("dp", None, None),
        check_vma=False,
    )
```

time: 204 us -> 136 us (0.67)
  Pallas kernels: 0 us -> 134 us
  waiting for transfers between devices: 88.2 us -> 0 us
  matrix products: 85 us -> 0 us
  other arithmetic: 13.4 us -> 0 us
  between operations: 13.4 us -> 0.01 us
    pallas_call x0 -> x1, Pallas kernels: none -> 134 us  [step(): pl.pallas_call(functools.partial(kernel, n), out_shape=jax.ShapeDtypeStru...]
    all_gather x1 -> x0, waiting for transfers between devices: 88.2 us -> none  [step(): return together(lax.all_gather(part_of(q, k, v), 'sp')).reshape(q.shape)]
    dot_general x2 -> x0, matrix products: 85 us -> none  [einsum(): return jnp.einsum(form, a.astype(jnp.float32), b.astype(jnp.float32))]
    reduce_sum x2 -> x0, other arithmetic: 9.6 us -> none  [the longest x1 8.59 us: together(): jnp.sum(seen * scale, 0) / jnp.sum(total * scale, 0)]
  transfers between devices with their start and end apart: 1 -> 0, of which waited for: 1 -> 0; matrix products, arithmetic and copies ran while one was open for 0% -> 0% of each run, Pallas kernels for 0% -> 0%
where the time goes in v1:
time: 136 us
  Pallas kernels  134 us (99%)
  local copies, waits for them, and re-layouts  1.82 us (1%)
    pallas_call x1, Pallas kernels, step(): pl.pallas_call(functools.partial(kernel, n), out_shape=jax.ShapeDtypeStru...  134 us

profile of v1, /device:TPU:0, one launch (start us, length us, event | category | flops | bytes accessed | tf_op | source)
XLA Modules:
  0.0 135.6 jit_solution(18357976871112810656)
XLA Ops:
  0.0 133.7 %shard_map.37 = bf16[32,56,128]{2,1,0:T(8,128)(2,1)} custom-call(bf16[32,56,128]{2,1,0:T(8,128)(2,1)} %q_hbm.1, bf16[32,128,7,16,128]{4,3,2,1,0:T(8,128)(2,1)} %bitcast.k_hbm, bf16[32,128,7,16,128]{4,3,2,1,0:T(8,128)(2,1)} %bitcast.1.v_hbm), custom_call_target="tpu_custom_call" | custom-call | tf_op jit(solution)/shard_map/pallas_call | solution.py:154
  133.7 1.8 %copy.5 = bf16[32,56,128]{2,1,0:T(8,128)(2,1)} copy(bf16[32,56,128]{2,1,0:T(8,128)(2,1)} %shard_map.37) | data formatting | bytes 917504

commit v2 on v1

v2 whole, which is shorter than its diff:
```python
import functools

import jax
import jax.numpy as jnp
from jax import lax
from jax.experimental import pallas as pl
from jax.experimental.pallas import tpu as pltpu
from jax.sharding import PartitionSpec as P

MESH = pl.DeviceIdType.MESH
LOG2E = 1.4426950408889634
SLOTS = 4
LAG = 3
ROWS = 16
TILE = 256
DELAY = 5


def kernel(
    n, q_hbm, k_hbm, v_hbm, o_hbm, kbuf, vbuf, qbuf, part, stat, part_in, stat_in, out,
    ksem, vsem, qsem, osem, done_sem, send_sem, recv_sem
):
    batch, half, _, groups, _, head = k_hbm.shape
    heads = q_hbm.shape[1]
    tiles = heads // 8
    me = lax.axis_index("sp")
    dp = lax.axis_index("dp")
    scale = head**-0.5 * LOG2E

    def fetch_k(b):
        slot = lax.rem(b, SLOTS)
        return pltpu.make_async_copy(k_hbm.at[b], kbuf.at[slot], ksem.at[slot])

    def fetch_v(b):
        slot = lax.rem(b, SLOTS)
        return pltpu.make_async_copy(v_hbm.at[b], vbuf.at[slot], vsem.at[slot])

    q_copy = pltpu.make_async_copy(q_hbm, qbuf, qsem)
    q_copy.start()
    for b in range(SLOTS):
        fetch_k(b).start()
        fetch_v(b).start()

    barrier = pltpu.get_barrier_semaphore()
    for i in range(1, n):
        pl.semaphore_signal(barrier, inc=1, device_id=(dp, lax.rem(me + i, n)), device_id_type=MESH)
    q_copy.wait()
    pl.semaphore_wait(barrier, n - 1)

    owned = batch - batch % n - n
    rounds = owned // n

    def seat(b):
        return jnp.where(b < owned, b // n, b - owned + rounds)

    def give(b, peer):
        for x, (ref, dst) in enumerate(((part, part_in), (stat, stat_in))):
            pltpu.make_async_remote_copy(
                src_ref=ref.at[b],
                dst_ref=dst.at[me, seat(b)],
                send_sem=send_sem.at[x],
                recv_sem=recv_sem.at[x, seat(b)],
                device_id=(dp, peer),
                device_id_type=MESH,
            ).start()

    def send(b):
        @pl.when((b < owned) & (lax.rem(b, n) != me))
        def _():
            give(b, lax.rem(b, n))

        @pl.when(b >= owned)
        def _():
            for i in range(1, n):
                give(b, lax.rem(me + i, n))

    def spread(b):
        for i in range(1, n):
            pltpu.make_async_remote_copy(
                src_ref=out.at[b],
                dst_ref=out.at[b],
                send_sem=send_sem.at[2],
                recv_sem=done_sem,
                device_id=(dp, lax.rem(me + i, n)),
                device_id_type=MESH,
            ).start()

    def finish(b):
        @pl.when((b >= owned) | (lax.rem(b, n) == me))
        def _():
            together(b)

        @pl.when((b < owned) & (lax.rem(b, n) == me))
        def _():
            spread(b)

    tiles_in = half * ROWS // TILE

    def tile_of(buf, slot, j, t):
        step = TILE // ROWS
        rows = [buf[slot, step * t : step * (t + 1), a, j].reshape(TILE, head) for a in range(2)]
        return jnp.concatenate(rows, 1)

    def eight(pieces, g):
        return pieces[8 * g // ROWS][8 * g % ROWS : 8 * g % ROWS + 8]

    def attend(b):
        q32 = qbuf[b].astype(jnp.float32)
        qq = jnp.concatenate([q32, q32], 0)
        row = lax.broadcasted_iota(jnp.int32, (2 * ROWS, TILE), 0) % ROWS
        col = lax.broadcasted_iota(jnp.int32, (2 * ROWS, TILE), 1) % ROWS
        own = row == col
        zero = jnp.zeros((ROWS, head), jnp.bfloat16)
        slot = lax.rem(b, SLOTS)
        pieces = range(tiles_in)
        sums, highs, totals, weights = {}, {}, {}, {}

        def score(j):
            q16 = qq[ROWS * j : ROWS * (j + 1)].astype(jnp.bfloat16)
            lhs = jnp.concatenate([jnp.concatenate([q16, zero], 1), jnp.concatenate([zero, q16], 1)], 0)
            s = {}
            for t in pieces:
                rhs = tile_of(kbuf, slot, j, t)
                s[t] = lax.dot_general(lhs, rhs, (((1,), (1,)), ((), ())), preferred_element_type=jnp.float32)
                s[t] = jnp.where(own, s[t], -jnp.inf)
            high = jnp.max(functools.reduce(jnp.maximum, s.values()), 1, keepdims=True)
            high = jnp.maximum(high[:ROWS], high[ROWS:])
            both = jnp.concatenate([high, high], 0)
            p = {t: jnp.exp2((s[t] - both) * scale) for t in s}
            total = jnp.sum(sum(p.values()), 1, keepdims=True)
            weights[j] = {t: p[t].astype(jnp.bfloat16) for t in p}
            highs[j], totals[j] = high, total[:ROWS] + total[ROWS:]

        def value(j):
            o = sum(
                jnp.dot(weights[j][t], tile_of(vbuf, slot, j, t), preferred_element_type=jnp.float32) for t in pieces
            )
            sums[j] = o[:ROWS, :head] + o[ROWS:, head:]

        for j in range(groups + DELAY):
            if j < groups:
                score(j)
            if j >= DELAY:
                value(j - DELAY)
        lane = lax.broadcasted_iota(jnp.int32, (8, head), 1)
        tile = jnp.zeros((8, head), jnp.float32)
        seen = []
        for g in range(tiles):
            h0, h1 = eight(highs, g), eight(highs, g + tiles)
            high = jnp.maximum(h0, h1)
            e0 = jnp.exp2((h0 - high) * scale)
            e1 = jnp.exp2((h1 - high) * scale)
            seen.append(eight(sums, g) * e0 + eight(sums, g + tiles) * e1)
            tile = jnp.where(lane == g, high, tile)
            tile = jnp.where(lane == g + 8, eight(totals, g) * e0 + eight(totals, g + tiles) * e1, tile)
        part[b] = jnp.concatenate(seen, 0).astype(jnp.bfloat16)
        stat[b] = tile

    def together(b):
        for x, ref in enumerate((part_in, stat_in)):
            peers = ref.at[pl.ds(0, n - 1), seat(b)]
            pltpu.make_async_copy(peers, peers, recv_sem.at[x, seat(b)]).wait()
        others = [lax.rem(me + i, n) for i in range(1, n)]
        stats = [stat[b]] + [stat_in[i, seat(b)] for i in others]
        high = functools.reduce(jnp.maximum, stats)
        weights = [jnp.exp2((s - high) * scale) for s in stats]
        total = sum(w * pltpu.roll(s, head - 8, 1) for w, s in zip(weights, stats))
        weights = [w / total for w in weights]
        acc = [jnp.zeros((8, head), jnp.float32)] * tiles
        for i in range(n):
            mine = (part_in[others[i - 1], seat(b)] if i else part[b]).astype(jnp.float32)
            for g in range(tiles):
                acc[g] = acc[g] + mine[8 * g : 8 * (g + 1)] * weights[i][:, g : g + 1]
        out[b] = jnp.concatenate(acc, 0).astype(jnp.bfloat16)

    def step(b, _):
        fetch_k(b).wait()
        fetch_v(b).wait()
        attend(b)
        send(b)

        @pl.when(b + SLOTS < batch)
        def _():
            fetch_k(b + SLOTS).start()
            fetch_v(b + SLOTS).start()

        @pl.when(b >= LAG)
        def _():
            finish(b - LAG)

        return 0

    lax.fori_loop(0, batch, step, 0)
    lax.fori_loop(batch - LAG, batch, lambda b, _: (finish(b), 0)[1], 0)
    for x, ref in enumerate((part_in, stat_in)):
        sent = ref.at[pl.ds(0, n - 1), pl.ds(0, rounds + n)]
        pltpu.make_async_copy(sent, sent, send_sem.at[x]).wait()
    sent = out.at[pl.ds(0, (n - 1) * rounds)]
    pltpu.make_async_copy(sent, sent, send_sem.at[2]).wait()
    pltpu.make_async_copy(sent, sent, done_sem).wait()
    copy = pltpu.make_async_copy(out, o_hbm, osem)
    copy.start()
    copy.wait()


def solution(mesh):
    n = mesh.shape["sp"]

    def step(q, k, v):
        batch, heads, head = q.shape
        tokens = k.shape[1]
        groups = 2 * heads // ROWS
        seats = batch // n - 1 + n
        shape = (batch, tokens // 4, 2, groups, ROWS, head)
        return pl.pallas_call(
            functools.partial(kernel, n),
            out_shape=jax.ShapeDtypeStruct(q.shape, q.dtype),
            in_specs=[pl.BlockSpec(memory_space=pl.ANY)] * 3,
            out_specs=pl.BlockSpec(memory_space=pl.ANY),
            scratch_shapes=[
                pltpu.VMEM((SLOTS,) + shape[1:], jnp.bfloat16),
                pltpu.VMEM((SLOTS,) + shape[1:], jnp.bfloat16),
                pltpu.VMEM(q.shape, jnp.bfloat16),
                pltpu.VMEM(q.shape, jnp.bfloat16),
                pltpu.VMEM((batch, 8, head), jnp.float32),
                pltpu.VMEM((n, seats, heads, head), jnp.bfloat16),
                pltpu.VMEM((n, seats, 8, head), jnp.float32),
                pltpu.VMEM(q.shape, jnp.bfloat16),
                pltpu.SemaphoreType.DMA((SLOTS,)),
                pltpu.SemaphoreType.DMA((SLOTS,)),
                pltpu.SemaphoreType.DMA,
                pltpu.SemaphoreType.DMA,
                pltpu.SemaphoreType.DMA,
                pltpu.SemaphoreType.DMA((3,)),
                pltpu.SemaphoreType.DMA((2, seats)),
            ],
            compiler_params=pltpu.CompilerParams(
                collective_id=0, has_side_effects=True, vmem_limit_bytes=60 * 1024 * 1024
            ),
        )(q, k.reshape(shape), v.reshape(shape))

    return jax.shard_map(
        step,
        mesh=mesh,
        in_specs=(P("dp", None, None), P("dp", "sp", None, None), P("dp", "sp", None, None)),
        out_specs=P("dp", None, None),
        check_vma=False,
    )
```

time: 136 us -> 81.4 us (0.60)
  Pallas kernels: 134 us -> 79.5 us
    pallas_call x1, Pallas kernels: 134 us -> 79.5 us  [step(): pl.pallas_call(functools.partial(kernel, n), out_shape=jax.ShapeDtypeStru...]
where the time goes in v2:
time: 81.4 us; the launch traced here: 81.3 us
  Pallas kernels  79.5 us (98%)
  local copies, waits for them, and re-layouts  1.82 us (2%)
    pallas_call x1, Pallas kernels, step(): pl.pallas_call(functools.partial(kernel, n), out_shape=jax.ShapeDtypeStru...  79.5 us
    unnamed x1, local copies, waits for them, and re-layouts  1.82 us

profile of v2, /device:TPU:0, one launch (start us, length us, event | category | flops | bytes accessed | tf_op | source)
XLA Modules:
  0.0 81.3 jit_solution(3770245554213818237)
XLA Ops:
  0.0 79.5 %shard_map.37 = bf16[32,56,128]{2,1,0:T(8,128)(2,1)} custom-call(bf16[32,56,128]{2,1,0:T(8,128)(2,1)} %q_hbm.1, bf16[32,64,2,7,16,128]{5,4,3,2,1,0:T(8,128)(2,1)} %bitcast.k_hbm, bf16[32,64,2,7,16,128]{5,4,3,2,1,0:T(8,128)(2,1)} %bitcast.1.v_hbm), custom_call_target="tpu_custom_call" | custom-call | tf_op jit(solution)/shard_map/pallas_call | solution.py:215
  79.5 1.8 %copy.5 = bf16[32,56,128]{2,1,0:T(8,128)(2,1)} copy(bf16[32,56,128]{2,1,0:T(8,128)(2,1)} %shard_map.37) | data formatting | bytes 917504

commit v3 on v2

v3 whole, which is shorter than its diff:
```python
import functools

import jax
import jax.numpy as jnp
from jax import lax
from jax.experimental import pallas as pl
from jax.experimental.pallas import tpu as pltpu
from jax.sharding import PartitionSpec as P

MESH = pl.DeviceIdType.MESH
LOG2E = 1.4426950408889634
LAG = 2
KEY_SLOTS = 4
VALUE_SLOTS = 3
TAIL = 2
ROWS = 16
TILE = 256
DELAY = 5


def kernel(
    n, q_hbm, k_hbm, v_hbm, out, kbuf, vbuf, qbuf, part, stat, part_in, stat_in,
    ksem, vsem, qsem, done_sem, spread_sem, give_sem, send_sem, recv_sem
):
    batch, half, _, groups, _, head = k_hbm.shape
    heads = q_hbm.shape[1]
    tiles = heads // 8
    me = lax.axis_index("sp")
    dp = lax.axis_index("dp")
    scale = head**-0.5 * LOG2E

    def fetch(hbm, buf, sem, b):
        slot = lax.rem(b, buf.shape[0])
        return pltpu.make_async_copy(hbm.at[b], buf.at[slot], sem.at[slot])

    def key_copy(b):
        return fetch(k_hbm, kbuf, ksem, b)

    def value_copy(b):
        return fetch(v_hbm, vbuf, vsem, b)

    q_copy = pltpu.make_async_copy(q_hbm, qbuf, qsem)
    q_copy.start()
    key_copy(0).start()
    value_copy(0).start()

    barrier = pltpu.get_barrier_semaphore()
    for i in range(1, n):
        pl.semaphore_signal(barrier, inc=1, device_id=(dp, lax.rem(me + i, n)), device_id_type=MESH)
    q_copy.wait()
    key_copy(1).start()
    value_copy(1).start()
    key_copy(2).start()
    pl.semaphore_wait(barrier, n - 1)

    owned = batch - TAIL
    rounds = -(-owned // n)

    def seat(b):
        return jnp.where(b < owned, b // n, b - owned + rounds)

    def give(x, b, peer, sem):
        ref, dst = ((part, part_in), (stat, stat_in))[x]
        pltpu.make_async_remote_copy(
            src_ref=ref.at[b],
            dst_ref=dst.at[me, seat(b)],
            send_sem=sem,
            recv_sem=recv_sem.at[x, seat(b)],
            device_id=(dp, peer),
            device_id_type=MESH,
        ).start()

    def give_owner(b):
        @pl.when(lax.rem(b, n) != me)
        def _():
            for x in range(2):
                give(x, b, lax.rem(b, n), give_sem.at[x, b])

    def give_all(x, b):
        for i in reversed(range(1, n)):
            give(x, b, lax.rem(me + i, n), send_sem.at[x])

    def spread(b):
        for i in range(1, n):
            pltpu.make_async_remote_copy(
                src_ref=out.at[b],
                dst_ref=out.at[b],
                send_sem=spread_sem.at[b],
                recv_sem=done_sem.at[b],
                device_id=(dp, lax.rem(me + i, n)),
                device_id_type=MESH,
            ).start()

    def finish(b):
        @pl.when(lax.rem(b, n) == me)
        def _():
            together(b)
            spread(b)

    tiles_in = half * ROWS // TILE

    def tile_of(buf, slot, j, t):
        step = TILE // ROWS
        rows = [buf[slot, step * t : step * (t + 1), a, j].reshape(TILE, head) for a in range(2)]
        return jnp.concatenate(rows, 1)

    def eight(pieces, g):
        return pieces[8 * g // ROWS][8 * g % ROWS : 8 * g % ROWS + 8]

    def attend(b, delay, between=None):
        q32 = qbuf[b].astype(jnp.float32)
        qq = jnp.concatenate([q32, q32], 0)
        row = lax.broadcasted_iota(jnp.int32, (2 * ROWS, TILE), 0) % ROWS
        col = lax.broadcasted_iota(jnp.int32, (2 * ROWS, TILE), 1) % ROWS
        own = row == col
        zero = jnp.zeros((ROWS, head), jnp.bfloat16)
        key_slot, value_slot = lax.rem(b, KEY_SLOTS), lax.rem(b, VALUE_SLOTS)
        pieces = range(tiles_in)
        sums, highs, totals, weights = {}, {}, {}, {}

        def score(j):
            q16 = qq[ROWS * j : ROWS * (j + 1)].astype(jnp.bfloat16)
            lhs = jnp.concatenate([jnp.concatenate([q16, zero], 1), jnp.concatenate([zero, q16], 1)], 0)
            s = {}
            for t in pieces:
                rhs = tile_of(kbuf, key_slot, j, t)
                s[t] = lax.dot_general(lhs, rhs, (((1,), (1,)), ((), ())), preferred_element_type=jnp.float32)
                s[t] = jnp.where(own, s[t], -jnp.inf)
            high = jnp.max(functools.reduce(jnp.maximum, s.values()), 1, keepdims=True)
            high = jnp.maximum(high[:ROWS], high[ROWS:])
            both = jnp.concatenate([high, high], 0)
            p = {t: jnp.exp2((s[t] - both) * scale) for t in s}
            total = jnp.sum(sum(p.values()), 1, keepdims=True)
            weights[j] = {t: p[t].astype(jnp.bfloat16) for t in p}
            highs[j], totals[j] = high, total[:ROWS] + total[ROWS:]

        def value(j):
            o = sum(
                jnp.dot(weights[j][t], tile_of(vbuf, value_slot, j, t), preferred_element_type=jnp.float32) for t in pieces
            )
            sums[j] = o[:ROWS, :head] + o[ROWS:, head:]

        ratios = {}

        def settle():
            lane = lax.broadcasted_iota(jnp.int32, (8, head), 1)
            tile = jnp.zeros((8, head), jnp.float32)
            for g in range(tiles):
                h0, h1 = eight(highs, g), eight(highs, g + tiles)
                high = jnp.maximum(h0, h1)
                e0 = jnp.exp2((h0 - high) * scale)
                e1 = jnp.exp2((h1 - high) * scale)
                tile = jnp.where(lane == g, high, tile)
                tile = jnp.where(lane == g + 8, eight(totals, g) * e0 + eight(totals, g + tiles) * e1, tile)
                ratios[g], ratios[g + tiles] = e0, e1
            stat[b] = tile

        for j in range(groups + delay):
            if j < groups:
                score(j)
            if j == groups and between is not None:
                settle()
                between()
            if j >= delay:
                value(j - delay)
        if between is None:
            settle()
        seen = [eight(sums, g) * ratios[g] + eight(sums, g + tiles) * ratios[g + tiles] for g in range(tiles)]
        part[b] = jnp.concatenate(seen, 0).astype(jnp.bfloat16)

    def together(b):
        for x, ref in enumerate((part_in, stat_in)):
            peers = ref.at[pl.ds(0, n - 1), seat(b)]
            pltpu.make_async_copy(peers, peers, recv_sem.at[x, seat(b)]).wait()
        others = [lax.rem(me + i, n) for i in range(1, n)]
        stats = [stat[b]] + [stat_in[i, seat(b)] for i in others]
        high = functools.reduce(jnp.maximum, stats)
        weights = [jnp.exp2((s - high) * scale) for s in stats]
        total = sum(w * pltpu.roll(s, head - 8, 1) for w, s in zip(weights, stats))
        weights = [w / total for w in weights]
        acc = [jnp.zeros((8, head), jnp.float32)] * tiles
        for i in range(n):
            mine = (part_in[others[i - 1], seat(b)] if i else part[b]).astype(jnp.float32)
            for g in range(tiles):
                acc[g] = acc[g] + mine[8 * g : 8 * (g + 1)] * weights[i][:, g : g + 1]
        out[b] = jnp.concatenate(acc, 0).astype(jnp.bfloat16)

    def step(b, _):
        key_copy(b).wait()
        value_copy(b).wait()

        @pl.when(b + 3 < batch)
        def _():
            key_copy(b + 3).start()

        attend(b, DELAY)
        value_copy(b + 2).start()
        give_owner(b)

        @pl.when(b >= LAG)
        def _():
            finish(b - LAG)

        return 0

    def last_step(b, _):
        key_copy(b).wait()

        def between():
            give_all(1, b)
            value_copy(b).wait()

        attend(b, groups, between)
        give_all(0, b)
        finish(b - LAG)
        return 0

    lax.fori_loop(0, owned, step, 0)
    lax.fori_loop(owned, batch, last_step, 0)
    def drain(b, _):
        @pl.when(lax.rem(b, n) == me)
        def _():
            sent = out.at[pl.ds(0, n - 1)]
            pltpu.make_async_copy(sent, sent, spread_sem.at[b]).wait()

        @pl.when(lax.rem(b, n) != me)
        def _():
            for x, ref in enumerate((part, stat)):
                pltpu.make_async_copy(ref.at[b], ref.at[b], give_sem.at[x, b]).wait()
            pltpu.make_async_copy(out.at[b], out.at[b], done_sem.at[b]).wait()

        return 0

    lax.fori_loop(0, owned, drain, 0)
    lax.fori_loop(owned, batch, lambda b, _: (together(b), 0)[1], 0)
    for x, ref in enumerate((part_in, stat_in)):
        sent = ref.at[pl.ds(0, n - 1), pl.ds(0, TAIL)]
        pltpu.make_async_copy(sent, sent, send_sem.at[x]).wait()


def solution(mesh):
    n = mesh.shape["sp"]

    def step(q, k, v):
        batch, heads, head = q.shape
        tokens = k.shape[1]
        groups = 2 * heads // ROWS
        seats = -(-(batch - TAIL) // n) + TAIL
        shape = (batch, tokens // 4, 2, groups, ROWS, head)
        return pl.pallas_call(
            functools.partial(kernel, n),
            out_shape=jax.ShapeDtypeStruct(q.shape, q.dtype),
            in_specs=[pl.BlockSpec(memory_space=pl.ANY)] * 3,
            out_specs=pl.BlockSpec(memory_space=pltpu.VMEM),
            scratch_shapes=[
                pltpu.VMEM((KEY_SLOTS,) + shape[1:], jnp.bfloat16),
                pltpu.VMEM((VALUE_SLOTS,) + shape[1:], jnp.bfloat16),
                pltpu.VMEM(q.shape, jnp.bfloat16),
                pltpu.VMEM(q.shape, jnp.bfloat16),
                pltpu.VMEM((batch, 8, head), jnp.float32),
                pltpu.VMEM((n, seats, heads, head), jnp.bfloat16),
                pltpu.VMEM((n, seats, 8, head), jnp.float32),
                pltpu.SemaphoreType.DMA((KEY_SLOTS,)),
                pltpu.SemaphoreType.DMA((VALUE_SLOTS,)),
                pltpu.SemaphoreType.DMA,
                pltpu.SemaphoreType.DMA((batch,)),
                pltpu.SemaphoreType.DMA((batch,)),
                pltpu.SemaphoreType.DMA((2, batch)),
                pltpu.SemaphoreType.DMA((2,)),
                pltpu.SemaphoreType.DMA((2, seats)),
            ],
            compiler_params=pltpu.CompilerParams(
                collective_id=0, has_side_effects=True, vmem_limit_bytes=40 * 1024 * 1024
            ),
        )(pltpu.with_memory_space_constraint(q, pltpu.HBM), k.reshape(shape), v.reshape(shape))

    return jax.shard_map(
        step,
        mesh=mesh,
        in_specs=(P("dp", None, None), P("dp", "sp", None, None), P("dp", "sp", None, None)),
        out_specs=P("dp", None, None),
        check_vma=False,
    )
```

time: 81.4 us -> 81 us (level)
  local copies, waits for them, and re-layouts: 1.82 us -> 0.77 us
    unnamed x1, local copies, waits for them, and re-layouts: 1.82 us -> 0.77 us
where the time goes in v3:
time: 81 us; the launch traced here: 80.9 us
  Pallas kernels  80.2 us (99%)
    pallas_call x1, Pallas kernels, step(): pl.pallas_call(functools.partial(kernel, n), out_shape=jax.ShapeDtypeStru...  80.2 us

profile of v3, /device:TPU:0, one launch (start us, length us, event | category | flops | bytes accessed | tf_op | source)
XLA Modules:
  0.0 80.9 jit_solution(7242738192258102170)
XLA Ops:
  0.0 80.2 %shard_map.37 = bf16[32,56,128]{2,1,0:T(8,128)(2,1)S(1)} custom-call(bf16[32,56,128]{2,1,0:T(8,128)(2,1)} %q_hbm.1, bf16[32,64,2,7,16,128]{5,4,3,2,1,0:T(8,128)(2,1)} %bitcast.k_hbm, bf16[32,64,2,7,16,128]{5,4,3,2,1,0:T(8,128)(2,1)} %bitcast.1.v_hbm), custom_call_target="tpu_custom_call" | custom-call | tf_op jit(solution)/shard_map/pallas_call | solution.py:250
  80.2 0.8 copy.5

commit v4 on v3

--- a/solution.py
+++ b/solution.py
@@ -10,7 +10,7 @@
 MESH = pl.DeviceIdType.MESH
 LOG2E = 1.4426950408889634
 LAG = 2
-KEY_SLOTS = 4
+KEY_SLOTS = 3
 VALUE_SLOTS = 3
 TAIL = 2
 ROWS = 16
@@ -50,7 +50,6 @@
     q_copy.wait()
     key_copy(1).start()
     value_copy(1).start()
-    key_copy(2).start()
     pl.semaphore_wait(barrier, n - 1)
 
     owned = batch - TAIL
@@ -70,15 +69,22 @@
             device_id_type=MESH,
         ).start()
 
+    x, y, core = me // 4, me // 2 % 2, me % 2
+    far_first = [
+        (x + dx) % 2 * 4 + (y + dy) % 2 * 2 + (core + dc) % 2
+        for dx, dy, dc in ((1, 1, 0), (1, 1, 1), (1, 0, 0), (0, 1, 0), (1, 0, 1), (0, 1, 1), (0, 0, 1))
+    ]
+
     def give_owner(b):
         @pl.when(lax.rem(b, n) != me)
         def _():
             for x in range(2):
                 give(x, b, lax.rem(b, n), give_sem.at[x, b])
 
-    def give_all(x, b):
-        for i in reversed(range(1, n)):
-            give(x, b, lax.rem(me + i, n), send_sem.at[x])
+    def give_all(b):
+        for peer in far_first:
+            for x in range(2):
+                give(x, b, peer, send_sem.at[x])
 
     def spread(b):
         for i in range(1, n):
@@ -107,7 +113,7 @@
     def eight(pieces, g):
         return pieces[8 * g // ROWS][8 * g % ROWS : 8 * g % ROWS + 8]
 
-    def attend(b, delay, between=None):
+    def attend(b):
         q32 = qbuf[b].astype(jnp.float32)
         qq = jnp.concatenate([q32, q32], 0)
         row = lax.broadcasted_iota(jnp.int32, (2 * ROWS, TILE), 0) % ROWS
@@ -155,16 +161,12 @@
                 ratios[g], ratios[g + tiles] = e0, e1
             stat[b] = tile
 
-        for j in range(groups + delay):
+        for j in range(groups + DELAY):
             if j < groups:
                 score(j)
-            if j == groups and between is not None:
-                settle()
-                between()
-            if j >= delay:
-                value(j - delay)
-        if between is None:
-            settle()
+            if j >= DELAY:
+                value(j - DELAY)
+        settle()
         seen = [eight(sums, g) * ratios[g] + eight(sums, g + tiles) * ratios[g + tiles] for g in range(tiles)]
         part[b] = jnp.concatenate(seen, 0).astype(jnp.bfloat16)
 
@@ -189,13 +191,20 @@
         key_copy(b).wait()
         value_copy(b).wait()
 
-        @pl.when(b + 3 < batch)
-        def _():
-            key_copy(b + 3).start()
-
-        attend(b, DELAY)
-        value_copy(b + 2).start()
-        give_owner(b)
+        @pl.when(b + 2 < batch)
+        def _():
+            key_copy(b + 2).start()
+            value_copy(b + 2).start()
+
+        attend(b)
+
+        @pl.when(b < owned)
+        def _():
+            give_owner(b)
+
+        @pl.when(b >= owned)
+        def _():
+            give_all(b)
 
         @pl.when(b >= LAG)
         def _():
@@ -203,20 +212,7 @@
 
         return 0
 
-    def last_step(b, _):
-        key_copy(b).wait()
-
-        def between():
-            give_all(1, b)
-            value_copy(b).wait()
-
-        attend(b, groups, between)
-        give_all(0, b)
-        finish(b - LAG)
-        return 0
-
-    lax.fori_loop(0, owned, step, 0)
-    lax.fori_loop(owned, batch, last_step, 0)
+    lax.fori_loop(0, batch, step, 0)
     def drain(b, _):
         @pl.when(lax.rem(b, n) == me)
         def _():

time: 81 us -> 79.4 us (0.980)
  Pallas kernels: 80.2 us -> 78.5 us
    pallas_call x1, Pallas kernels: 80.2 us -> 78.5 us  [step(): pl.pallas_call(functools.partial(kernel, n), out_shape=jax.ShapeDtypeStru...]
where the time goes in v4:
time: 79.4 us; the launch traced here: 79.3 us
  Pallas kernels  78.5 us (99%)
    pallas_call x1, Pallas kernels, step(): pl.pallas_call(functools.partial(kernel, n), out_shape=jax.ShapeDtypeStru...  78.5 us

profile of v4, /device:TPU:0, one launch (start us, length us, event | category | flops | bytes accessed | tf_op | source)
XLA Modules:
  0.0 79.3 jit_solution(7599798983205870584)
XLA Ops:
  0.0 78.5 %shard_map.37 = bf16[32,56,128]{2,1,0:T(8,128)(2,1)S(1)} custom-call(bf16[32,56,128]{2,1,0:T(8,128)(2,1)} %q_hbm.1, bf16[32,64,2,7,16,128]{5,4,3,2,1,0:T(8,128)(2,1)} %bitcast.k_hbm, bf16[32,64,2,7,16,128]{5,4,3,2,1,0:T(8,128)(2,1)} %bitcast.1.v_hbm), custom_call_target="tpu_custom_call" | custom-call | tf_op jit(solution)/shard_map/pallas_call | solution.py:246
  78.5 0.8 copy.5

commit v5 on v4

--- a/solution.py
+++ b/solution.py
@@ -10,16 +10,16 @@
 MESH = pl.DeviceIdType.MESH
 LOG2E = 1.4426950408889634
 LAG = 2
-KEY_SLOTS = 3
-VALUE_SLOTS = 3
-TAIL = 2
+LEAD = 2
+SLOTS = 3
+TAIL = 4
 ROWS = 16
 TILE = 256
-DELAY = 5
+DELAY = 7
 
 
 def kernel(
-    n, q_hbm, k_hbm, v_hbm, out, kbuf, vbuf, qbuf, part, stat, part_in, stat_in,
+    n, q_hbm, k_hbm, v_hbm, out, kbuf, vbuf, qbuf, w0, w1, w2, r0, r1, r2, part, stat, part_in, stat_in,
     ksem, vsem, qsem, done_sem, spread_sem, give_sem, send_sem, recv_sem
 ):
     batch, half, _, groups, _, head = k_hbm.shape
@@ -41,15 +41,13 @@
 
     q_copy = pltpu.make_async_copy(q_hbm, qbuf, qsem)
     q_copy.start()
-    key_copy(0).start()
-    value_copy(0).start()
+    for b in range(SLOTS):
+        key_copy(b).start()
 
     barrier = pltpu.get_barrier_semaphore()
     for i in range(1, n):
         pl.semaphore_signal(barrier, inc=1, device_id=(dp, lax.rem(me + i, n)), device_id_type=MESH)
     q_copy.wait()
-    key_copy(1).start()
-    value_copy(1).start()
     pl.semaphore_wait(barrier, n - 1)
 
     owned = batch - TAIL
@@ -75,16 +73,14 @@
         for dx, dy, dc in ((1, 1, 0), (1, 1, 1), (1, 0, 0), (0, 1, 0), (1, 0, 1), (0, 1, 1), (0, 0, 1))
     ]
 
-    def give_owner(b):
+    def give_owner(x, b):
         @pl.when(lax.rem(b, n) != me)
         def _():
-            for x in range(2):
-                give(x, b, lax.rem(b, n), give_sem.at[x, b])
-
-    def give_all(b):
+            give(x, b, lax.rem(b, n), give_sem.at[x, b])
+
+    def give_all(x, b):
         for peer in far_first:
-            for x in range(2):
-                give(x, b, peer, send_sem.at[x])
+            give(x, b, peer, send_sem.at[x])
 
     def spread(b):
         for i in range(1, n):
@@ -103,6 +99,7 @@
             together(b)
             spread(b)
 
+    weight_bufs, ratio_bufs = (w0, w1, w2), (r0, r1, r2)
     tiles_in = half * ROWS // TILE
 
     def tile_of(buf, slot, j, t):
@@ -113,16 +110,12 @@
     def eight(pieces, g):
         return pieces[8 * g // ROWS][8 * g % ROWS : 8 * g % ROWS + 8]
 
-    def attend(b):
-        q32 = qbuf[b].astype(jnp.float32)
-        qq = jnp.concatenate([q32, q32], 0)
-        row = lax.broadcasted_iota(jnp.int32, (2 * ROWS, TILE), 0) % ROWS
-        col = lax.broadcasted_iota(jnp.int32, (2 * ROWS, TILE), 1) % ROWS
-        own = row == col
-        zero = jnp.zeros((ROWS, head), jnp.bfloat16)
-        key_slot, value_slot = lax.rem(b, KEY_SLOTS), lax.rem(b, VALUE_SLOTS)
+    def stage(b, x, scoring, summing):
+        key_slot, value_slot = lax.rem(b, SLOTS), lax.rem(b - LEAD + SLOTS, SLOTS)
+        wbuf, ebuf = weight_bufs[x], ratio_bufs[x]
+        old_wbuf, old_ebuf = weight_bufs[(x + 1) % SLOTS], ratio_bufs[(x + 1) % SLOTS]
         pieces = range(tiles_in)
-        sums, highs, totals, weights = {}, {}, {}, {}
+        sums, highs, totals = {}, {}, {}
 
         def score(j):
             q16 = qq[ROWS * j : ROWS * (j + 1)].astype(jnp.bfloat16)
@@ -137,18 +130,30 @@
             both = jnp.concatenate([high, high], 0)
             p = {t: jnp.exp2((s[t] - both) * scale) for t in s}
             total = jnp.sum(sum(p.values()), 1, keepdims=True)
-            weights[j] = {t: p[t].astype(jnp.bfloat16) for t in p}
+            for t in p:
+                wbuf[j, t] = p[t].astype(jnp.bfloat16)
             highs[j], totals[j] = high, total[:ROWS] + total[ROWS:]
 
         def value(j):
             o = sum(
-                jnp.dot(weights[j][t], tile_of(vbuf, value_slot, j, t), preferred_element_type=jnp.float32) for t in pieces
+                jnp.dot(old_wbuf[j, t], tile_of(vbuf, value_slot, j, t), preferred_element_type=jnp.float32)
+                for t in pieces
             )
             sums[j] = o[:ROWS, :head] + o[ROWS:, head:]
 
-        ratios = {}
-
-        def settle():
+        if scoring:
+            q32 = qbuf[b].astype(jnp.float32)
+            qq = jnp.concatenate([q32, q32], 0)
+            row = lax.broadcasted_iota(jnp.int32, (2 * ROWS, TILE), 0) % ROWS
+            col = lax.broadcasted_iota(jnp.int32, (2 * ROWS, TILE), 1) % ROWS
+            own = row == col
+            zero = jnp.zeros((ROWS, head), jnp.bfloat16)
+        for j in range(groups + DELAY):
+            if scoring and j < groups:
+                score(j)
+            if summing and j >= DELAY:
+                value(j - DELAY)
+        if scoring:
             lane = lax.broadcasted_iota(jnp.int32, (8, head), 1)
             tile = jnp.zeros((8, head), jnp.float32)
             for g in range(tiles):
@@ -156,19 +161,14 @@
                 high = jnp.maximum(h0, h1)
                 e0 = jnp.exp2((h0 - high) * scale)
                 e1 = jnp.exp2((h1 - high) * scale)
+                ebuf[g] = jnp.broadcast_to(e0, (8, head))
+                ebuf[g + tiles] = jnp.broadcast_to(e1, (8, head))
                 tile = jnp.where(lane == g, high, tile)
                 tile = jnp.where(lane == g + 8, eight(totals, g) * e0 + eight(totals, g + tiles) * e1, tile)
-                ratios[g], ratios[g + tiles] = e0, e1
             stat[b] = tile
-
-        for j in range(groups + DELAY):
-            if j < groups:
-                score(j)
-            if j >= DELAY:
-                value(j - DELAY)
-        settle()
-        seen = [eight(sums, g) * ratios[g] + eight(sums, g + tiles) * ratios[g + tiles] for g in range(tiles)]
-        part[b] = jnp.concatenate(seen, 0).astype(jnp.bfloat16)
+        if summing:
+            seen = [eight(sums, g) * old_ebuf[g] + eight(sums, g + tiles) * old_ebuf[g + tiles] for g in range(tiles)]
+            part[b - LEAD] = jnp.concatenate(seen, 0).astype(jnp.bfloat16)
 
     def together(b):
         for x, ref in enumerate((part_in, stat_in)):
@@ -187,32 +187,49 @@
                 acc[g] = acc[g] + mine[8 * g : 8 * (g + 1)] * weights[i][:, g : g + 1]
         out[b] = jnp.concatenate(acc, 0).astype(jnp.bfloat16)
 
-    def step(b, _):
+    def share(x, b):
+        @pl.when(b < owned)
+        def _():
+            give_owner(x, b)
+
+        @pl.when(b >= owned)
+        def _():
+            give_all(x, b)
+
+    def step(b, x):
         key_copy(b).wait()
-        value_copy(b).wait()
+        value_copy(b - LEAD).wait()
 
         @pl.when(b + 2 < batch)
         def _():
             key_copy(b + 2).start()
-            value_copy(b + 2).start()
-
-        attend(b)
-
-        @pl.when(b < owned)
-        def _():
-            give_owner(b)
-
-        @pl.when(b >= owned)
-        def _():
-            give_all(b)
-
-        @pl.when(b >= LAG)
-        def _():
-            finish(b - LAG)
-
+
+        value_copy(b).start()
+        stage(b, x, True, True)
+        share(0, b - LEAD)
+        share(1, b)
+
+        @pl.when(b >= LEAD + LAG)
+        def _():
+            finish(b - LEAD - LAG)
+
+    def steps(i, _):
+        for u in range(SLOTS):
+            step(LEAD + SLOTS * i + u, (LEAD + u) % SLOTS)
         return 0
 
-    lax.fori_loop(0, batch, step, 0)
+    for b in range(LEAD):
+        key_copy(b).wait()
+        if b:
+            key_copy(b + 2).start()
+        value_copy(b).start()
+        stage(b, b, True, False)
+        give_owner(1, b)
+    lax.fori_loop(0, (batch - LEAD) // SLOTS, steps, 0)
+    for b in range(batch, batch + LEAD):
+        value_copy(b - LEAD).wait()
+        stage(b, b % SLOTS, False, True)
+        give_all(0, b - LEAD)
     def drain(b, _):
         @pl.when(lax.rem(b, n) == me)
         def _():
@@ -249,15 +266,17 @@
             in_specs=[pl.BlockSpec(memory_space=pl.ANY)] * 3,
             out_specs=pl.BlockSpec(memory_space=pltpu.VMEM),
             scratch_shapes=[
-                pltpu.VMEM((KEY_SLOTS,) + shape[1:], jnp.bfloat16),
-                pltpu.VMEM((VALUE_SLOTS,) + shape[1:], jnp.bfloat16),
+                pltpu.VMEM((SLOTS,) + shape[1:], jnp.bfloat16),
+                pltpu.VMEM((SLOTS,) + shape[1:], jnp.bfloat16),
                 pltpu.VMEM(q.shape, jnp.bfloat16),
+                *[pltpu.VMEM((groups, tokens // 4 * ROWS // TILE, 2 * ROWS, TILE), jnp.bfloat16)] * SLOTS,
+                *[pltpu.VMEM((groups * ROWS // 8, 8, head), jnp.float32)] * SLOTS,
                 pltpu.VMEM(q.shape, jnp.bfloat16),
                 pltpu.VMEM((batch, 8, head), jnp.float32),
                 pltpu.VMEM((n, seats, heads, head), jnp.bfloat16),
                 pltpu.VMEM((n, seats, 8, head), jnp.float32),
-                pltpu.SemaphoreType.DMA((KEY_SLOTS,)),
-                pltpu.SemaphoreType.DMA((VALUE_SLOTS,)),
+                pltpu.SemaphoreType.DMA((SLOTS,)),
+                pltpu.SemaphoreType.DMA((SLOTS,)),
                 pltpu.SemaphoreType.DMA,
                 pltpu.SemaphoreType.DMA((batch,)),
                 pltpu.SemaphoreType.DMA((batch,)),

time: 79.4 us -> 79.9 us (level)
  no operation moved by 1% of the time
where the time goes in v5:
time: 79.9 us; the launch traced here: 79.8 us
  Pallas kernels  79 us (99%)
    pallas_call x1, Pallas kernels, step(): pl.pallas_call(functools.partial(kernel, n), out_shape=jax.ShapeDtypeStru...  79 us

profile of v5, /device:TPU:0, one launch (start us, length us, event | category | flops | bytes accessed | tf_op | source)
XLA Modules:
  0.0 79.8 jit_solution(12703125415305228831)
XLA Ops:
  0.0 79.0 %shard_map.37 = bf16[32,56,128]{2,1,0:T(8,128)(2,1)S(1)} custom-call(bf16[32,56,128]{2,1,0:T(8,128)(2,1)} %q_hbm.1, bf16[32,64,2,7,16,128]{5,4,3,2,1,0:T(8,128)(2,1)} %bitcast.k_hbm, bf16[32,64,2,7,16,128]{5,4,3,2,1,0:T(8,128)(2,1)} %bitcast.1.v_hbm), custom_call_target="tpu_custom_call" | custom-call | tf_op jit(solution)/shard_map/pallas_call | solution.py:263
  79.0 0.8 copy.5
